TPU v7x, 32 devices: a whole 2x2x4 slice. The times are simulated.
32 devices in a mesh: groups: 2 (over x), cent: 16 (over z, y, core).
Axes of the slice: x: 2, y: 2, z: 4, core: 2. Of those that a mesh axis runs over, the one named last changes fastest.
Arguments:
- points: bfloat16 [1024, 768], P(('groups', 'cent')), parts along dimension 0, may hold values from -64 to 64, as said below
- centroids: bfloat16 [131072, 768], P(('groups', 'cent')), parts along dimension 0, may hold values from -1 to 1
- coarse_init: float32 [4096, 768], P(('groups', 'cent')), parts along dimension 0, may hold values from -2.4 to 2.4
- assign: int32 [131072], P(('groups', 'cent')), parts along dimension 0, may hold values from 0 to 2047, as said below
Outputs:
- level_one: bfloat16 [131072, 768], P(('groups', 'cent')), parts along dimension 0
- level_two: float32 [4096, 768], P(('groups', 'cent')), parts along dimension 0
There are 2 independent parts, one for each index of `groups`. A program takes and returns all parts, laid end to end along the dimension named above; each array names one. Nothing has to cross between parts.
Inputs may be any that keep to these rules, and one draw needn't show every extreme that they name: `points`: entries normal (clipped at 8) or uniform within 1.7; on some draws a few rows are scaled multiples of a centroid that has a close twin, giving logits up to about 300. `assign`: among the 65536 // 16 level-1 centroids held by one index of cent, at most 512 have their level-2 centroid in any one block of 2048 // 16 consecutive level-2 centroids, and some block receives exactly 512.
All inputs are finite; a program needn't handle non-finite values.
Results may differ from a plain program's by a relative error of at most 0.0039.
Values may be sent and summed in bfloat16 or wider, within the bound.
A program may use at most 64 MiB of HBM per device.

v0:
```python
import math

import jax
import jax.numpy as jnp
from jax import lax
from jax.sharding import PartitionSpec as P

D = 768
K2 = 2048


TEMP = 0.05
PRIOR_ONE = 0.02
PRIOR_TWO = 0.25


def shards(points, centroids, coarse_init, assign):
    scale = 1.0 / (TEMP * math.sqrt(D))
    everyone = lax.all_gather(points, "cent", axis=0, tiled=True)
    count = everyone.shape[0]
    rows = min(512, count)
    pblocks = everyone.reshape(count // rows, rows, D)
    local_k = centroids.shape[0]

    def logits_of(block):
        return (
            lax.dot_general(
                block, centroids, (((1,), (1,)), ((), ())), preferred_element_type=jnp.float32
            )
            * scale
        )

    def local_stats(block):
        logits = logits_of(block)
        top = jnp.max(logits, axis=1)
        return (top, jnp.sum(jnp.exp(logits - top[:, None]), axis=1))

    local_top, local_sum = lax.map(local_stats, pblocks)
    local_top = local_top.reshape(count)
    local_sum = local_sum.reshape(count)
    peak = lax.pmax(local_top, "cent")
    total = lax.psum(local_sum * jnp.exp(local_top - peak), "cent")
    peaks = peak.reshape(count // rows, rows)
    totals = total.reshape(count // rows, rows)

    def accumulate(carry, item):
        block, peak_rows, total_rows = item
        resp = jnp.exp(logits_of(block) - peak_rows[:, None]) / total_rows[:, None]
        mass = carry[0] + jnp.sum(resp, axis=0)
        weighted = carry[1] + lax.dot_general(
            resp.astype(jnp.bfloat16),
            block,
            (((0,), (0,)), ((), ())),
            preferred_element_type=jnp.float32,
        )
        return ((mass, weighted), None)

    start_carry = (jnp.zeros((local_k,), jnp.float32), jnp.zeros((local_k, D), jnp.float32))
    (mass, weighted), _ = lax.scan(accumulate, start_carry, (pblocks, peaks, totals))
    fresh = (weighted + PRIOR_ONE * centroids.astype(jnp.float32)) / (mass[:, None] + PRIOR_ONE)
    level_one = fresh.astype(jnp.bfloat16)
    moved = (mass[:, None] * fresh).astype(jnp.bfloat16)
    mass_high = mass.astype(jnp.bfloat16)
    mass_low = (mass - mass_high.astype(jnp.float32)).astype(jnp.bfloat16)
    onehot = (assign[:, None] == lax.broadcasted_iota(jnp.int32, (1, K2), 1)).astype(jnp.bfloat16)
    wsum_term = lax.dot_general(
        onehot, moved, (((0,), (0,)), ((), ())), preferred_element_type=jnp.float32
    )
    mass_pair = jnp.stack([mass_high, mass_low])
    msum_term = jnp.sum(jnp.dot(mass_pair, onehot, preferred_element_type=jnp.float32), axis=0)
    wsum, msum = (
        lax.psum_scatter(wsum_term, "cent", scatter_dimension=0, tiled=True),
        lax.psum_scatter(msum_term, "cent", scatter_dimension=0, tiled=True),
    )
    level_two = (wsum + PRIOR_TWO * coarse_init) / (msum[:, None] + PRIOR_TWO)
    return (level_one, level_two)


def solution(mesh):
    return jax.shard_map(
        shards,
        mesh=mesh,
        in_specs=(
            P(("groups", "cent"), None),
            P(("groups", "cent"), None),
            P(("groups", "cent"), None),
            P(("groups", "cent")),
        ),
        out_specs=(P(("groups", "cent"), None), P(("groups", "cent"), None)),
        check_vma=False,
    )
```

profile of v0, /device:TPU:10, one launch (start us, length us, event | category | flops | bytes accessed | tf_op | source)
XLA Modules:
  0.0 234.3 jit_solution(16250268285683801577)
XLA Ops:
  7.2 0.0 reduce-scatter.2.cloned.1.call-start
  7.2 21.3 %all_gather.3 = bf16[512,768]{1,0:T(8,128)(2,1)S(1)} all-gather(bf16[32,768]{1,0:T(8,128)(2,1)} %param.4), channel_id=1, replica_groups=mesh['groups'=2,'cent'=16] {'cent'}, dimensions={0}, use_global_device_ids=true | all-gather | bytes 835584 | tf_op jit(solution)/shard_map/all_gather | solution.py:19
  28.6 8.4 %multiply_reduce_fusion = (f32[512]{0:T(512)S(1)}, f32[512,4096]{1,0:T(8,128)}) fusion(bf16[512,768]{1,0:T(8,128)(2,1)S(1)} %all_gather.3, bf16[4096,768]{1,0:T(8,128)(2,1)} %param.5), kind=kOutput, calls=%fused_computation.9 | convolution fusion | flops 3225419264 | bytes 15468544 | tf_op jit(solution)/shard_map/while/body/eval_jaxpr/dot_general | solution.py:27
  37.0 24.7 %pmax.7 = f32[512]{0:T(512)S(1)} all-reduce(f32[512]{0:T(512)S(1)} %get-tuple-element.24), channel_id=1, replica_groups=mesh['groups'=2,'cent'=16] {'cent'}, use_global_device_ids=true, to_apply=%region_1.0 | all-reduce | flops 512 | bytes 4096 | tf_op jit(solution)/shard_map/pmax | solution.py:41
  61.7 4.9 %exponential_reduce_fusion = f32[512]{0:T(512)S(1)} fusion(f32[512,4096]{1,0:T(8,128)} %get-tuple-element.25, f32[512]{0:T(512)S(1)} %get-tuple-element.24), kind=kLoop, calls=%fused_computation.7 | loop fusion | flops 6290944 | bytes 8392704 | tf_op jit(solution)/shard_map/while/body/eval_jaxpr/reduce_sum | solution.py:36
  66.6 29.5 %psum.7 = f32[512]{0:T(512)S(1)} all-reduce(f32[512]{0:T(512)S(1)} %exponential_multiply_fusion), channel_id=1, replica_groups=mesh['groups'=2,'cent'=16] {'cent'}, use_global_device_ids=true, to_apply=%region_3.4 | all-reduce | flops 512 | bytes 4096 | tf_op jit(solution)/shard_map/psum | solution.py:42
  96.1 4.5 %fusion.11 = f32[4096]{0:T(1024)S(1)} fusion(f32[512]{0:T(512)S(1)} %psum.7, f32[512]{0:T(512)S(1)} %pmax.7, f32[512,4096]{1,0:T(8,128)} %get-tuple-element.25), kind=kLoop, calls=%fused_computation.22 | loop fusion | flops 8384512 | bytes 8409088 | tf_op jit(solution)/shard_map/while/body/eval_jaxpr/reduce_sum | solution.py:49
  100.6 0.0 copy-start.1
  100.6 12.1 %fusion.12 = (bf16[4096,768]{1,0:T(8,128)(2,1)}, f32[4096,768]{1,0:T(8,128)}) fusion(f32[4096]{0:T(1024)S(1)} %broadcast_add_fusion, bf16[4096,768]{1,0:T(8,128)(2,1)} %param.5, bf16[512,768]{1,0:T(8,128)(2,1)S(1)} %all_gather.3, f32[512]{0:T(512)S(1)} %psum.7, f32[512]{0:T(512)S(1)} %pmax.7, f32[512,4096]{1,0:T(8,128)} %get-tuple-element.25), kind=kOutput, calls=%fused_computation.23 | convolution fusion | flops 3245342720 | bytes 34361344 | tf_op jit(solution)/shard_map/while/body/eval_jaxpr/dot_general | solution.py:50
  112.7 0.0 copy-done.1
  112.7 0.0 copy-start.2
  112.7 22.7 %fusion.1 = f32[2048,768]{1,0:T(8,128)} fusion(s32[4096]{0:T(1024)S(1)} %copy-done.1, f32[4096,768]{1,0:T(8,128)} %get-tuple-element.34, f32[4096]{0:T(1024)S(1)} %fusion.11), kind=kOutput, calls=%fused_computation.2 | convolution fusion | flops 12899581952 | bytes 18907136 | tf_op jit(solution)/shard_map/dot_general | solution.py:66
  135.4 0.0 copy-start
  135.4 0.0 reduce-scatter.2.cloned.1.call-update
  135.5 0.0 copy-done.2
  135.5 0.6 dynamic-slice.3
  136.7 5.9 %fusion.6 = f32[2048]{0:T(1024)S(1)} fusion(s32[4096]{0:T(1024)S(1)} %copy-done.1, bf16[1,4096]{1,0:T(2,128)(2,1)S(1)} %subtract_convert_fusion, bf16[1,4096]{1,0:T(2,128)(2,1)S(1)} %convert_element_type.52), kind=kOutput, calls=%fused_computation.12 | convolution fusion | flops 41977856 | bytes 40960 | tf_op jit(solution)/shard_map/dot_general | solution.py:70
  142.6 29.9 %all-reduce = f32[2048]{0:T(1024)S(1)} all-reduce(f32[2048]{0:T(1024)S(1)} %fusion.6), channel_id=3, replica_groups=mesh['groups'=2,'cent'=16] {'cent'}, use_global_device_ids=true, to_apply=%region_7.8.clone | all-reduce | flops 2048 | bytes 16384
  172.5 0.1 dynamic-slice_add_fusion
  172.6 53.0 %reduce-scatter.2.cloned.1.call-done = f32[128,768]{1,0:T(8,128)} async-done(((f32[2048,768]{1,0:T(8,128)}), f32[128,768]{1,0:T(8,128)}) %reduce-scatter.2.cloned.1.call-update) | async-done | bytes 393232 | tf_op jit(solution)/shard_map/reduce_scatter | solution.py:72
  225.6 0.0 copy-done
  225.6 1.8 add_divide_fusion.1
  (4 shorter events, 0.0 us)
Async XLA Ops:
  7.2 218.4 %reduce-scatter.2.cloned.1.call-start = ((), (), s32[]{:S(2)}) async-start(), calls=%async_computation.1 | async-start | bytes 6684672 | tf_op jit(solution)/shard_map/reduce_scatter | solution.py:72
  100.6 12.1 %copy-start.1 = (s32[4096]{0:T(1024)S(1)}, s32[4096]{0:T(1024)}, u32[]{:S(2)}) copy-start(s32[4096]{0:T(1024)} %param.7) | copy-start | bytes 49156
  112.7 22.8 %copy-start.2 = (u32[32]{0:T(128)S(1)}, u32[32]{0:T(128)}, u32[]{:S(2)}) copy-start(u32[32]{0:T(128)} %constant.43) | copy-start | bytes 388
  135.4 90.2 %copy-start = (f32[128,768]{1,0:T(8,128)S(1)}, f32[128,768]{1,0:T(8,128)}, u32[]{:S(2)}) copy-start(f32[128,768]{1,0:T(8,128)} %param.6) | copy-start | bytes 1179652
Sparse Core Ops, SparseCore 0:
  135.5 90.0 reduce-scatter.1
where the time goes:
time: 237 us; the launch traced here: 234 us
  blocking collectives  105 us (44%)
  waiting for transfers between devices  53 us (22%)
  matrix products  49.1 us (21%)
  between operations  14.8 us (6%)
  other arithmetic  11.3 us (5%)
    reduce_scatter x1, waiting for transfers between devices, shards(): lax.psum_scatter(wsum_term, 'cent', scatter_dimension=0, tiled=True)  53 us
    unnamed x1, blocking collectives  29.9 us
    psum x1, blocking collectives, shards(): total = lax.psum(local_sum * jnp.exp(local_top - peak), 'cent')  29.5 us
    pmax x1, blocking collectives, shards(): peak = lax.pmax(local_top, 'cent')  24.7 us
    dot_general x1, matrix products, shards(): lax.dot_general(onehot, moved, (((0,), (0,)), ((), ())), preferred_elemen...  22.7 us
    all_gather x1, blocking collectives, shards(): everyone = lax.all_gather(points, 'cent', axis=0, tiled=True)  21.3 us
    dot_general x1, matrix products, accumulate(): lax.dot_general(resp.astype(jnp.bfloat16), block, (((0,), (0,)), ((), ())...  12.1 us
    dot_general x1, matrix products, logits_of(): lax.dot_general(block, centroids, (((1,), (1,)), ((), ())), preferred_ele...  8.45 us
  transfers between devices with their start and end apart: 1, of which 1 were waited for; matrix products, arithmetic and copies ran while one was open for 3% of the time, Pallas kernels for 0%

commit v1 on v0

v1 whole, which is shorter than its diff:
```python
import functools
import math

import jax
import jax.numpy as jnp
from jax import lax
from jax.experimental import pallas as pl
from jax.experimental.pallas import tpu as pltpu
from jax.sharding import PartitionSpec as P

TEMP = 0.05
PRIOR_ONE = 0.02
PRIOR_TWO = 0.25
LANES = 128
MESH = pl.DeviceIdType.MESH
ROWS_BY_ROWS = (((1,), (1,)), ((), ()))


def log2_scale(width):
    return math.log2(math.e) / (TEMP * math.sqrt(width))


def stats_kernel(n, tile, pts_ref, cen_hbm, all_ref, lse_ref, cen, mine, theirs, cen_sem, sems):
    group, me = lax.axis_index("groups"), lax.axis_index("cent")
    rows, width = pts_ref.shape
    count = all_ref.shape[0]
    tiles = cen.shape[0] // tile
    c2 = log2_scale(width)

    def fetch(t):
        part = pl.ds(t * tile, tile)
        return pltpu.make_async_copy(cen_hbm.at[part], cen.at[part], cen_sem.at[t])

    for t in range(tiles):
        fetch(t).start()

    barrier = pltpu.get_barrier_semaphore()

    @pl.loop(1, n)
    def _(off):
        peer = lax.rem(me + off, n)
        pl.semaphore_signal(barrier, inc=1, device_id=(group, peer), device_id_type=MESH)

    pl.semaphore_wait(barrier, n - 1)

    here = pl.ds(pl.multiple_of(me * rows, rows), rows)

    @pl.loop(1, n)
    def _(off):
        pltpu.make_async_remote_copy(
            src_ref=pts_ref,
            dst_ref=all_ref.at[here],
            send_sem=sems.at[0],
            recv_sem=sems.at[1],
            device_id=(group, lax.rem(me + off, n)),
            device_id_type=MESH,
        ).start()

    all_ref[here, :] = pts_ref[...]
    others = all_ref.at[pl.ds(0, (n - 1) * rows)]
    pltpu.make_async_copy(others, others, sems.at[1]).wait()

    peak = jnp.full((1, count), -jnp.inf, jnp.float32)
    total = jnp.zeros((1, count), jnp.float32)

    def step(t, carry):
        peak, total = carry
        fetch(t).wait()
        block = cen[pl.ds(pl.multiple_of(t * tile, tile), tile), :]
        logits = (
            lax.dot_general(block, all_ref[...], ROWS_BY_ROWS, preferred_element_type=jnp.float32)
            * c2
        )
        higher = jnp.maximum(peak, jnp.max(logits, axis=0, keepdims=True))
        total = total * jnp.exp2(peak - higher) + jnp.sum(
            jnp.exp2(logits - higher), axis=0, keepdims=True
        )
        return higher, total

    peak, total = lax.fori_loop(0, tiles, step, (peak, total))
    mine[0:1, :] = peak
    mine[1:2, :] = total

    @pl.loop(1, n)
    def _(off):
        pltpu.make_async_remote_copy(
            src_ref=mine,
            dst_ref=theirs.at[off - 1],
            send_sem=sems.at[2],
            recv_sem=sems.at[3],
            device_id=(group, lax.rem(me + off, n)),
            device_id_type=MESH,
        ).start()

    pltpu.make_async_copy(theirs, theirs, sems.at[3]).wait()
    both = theirs[...]
    top = jnp.maximum(peak, jnp.max(both[:, 0:1, :], axis=0))
    denom = total * jnp.exp2(peak - top) + jnp.sum(
        both[:, 1:2, :] * jnp.exp2(both[:, 0:1, :] - top[None]), axis=0
    )
    lse_ref[...] = top + jnp.log2(denom)
    pltpu.make_async_copy(others, others, sems.at[0]).wait()
    pltpu.make_async_copy(theirs, theirs, sems.at[2]).wait()


def update_kernel(cen_ref, pts_ref, lse_ref, one_ref, moved_ref, mass_ref):
    tile, width = cen_ref.shape
    cen, pts = cen_ref[...], pts_ref[...]
    logits = lax.dot_general(cen, pts, ROWS_BY_ROWS, preferred_element_type=jnp.float32)
    resp = jnp.exp2(logits * log2_scale(width) - lse_ref[...])
    mass = jnp.sum(resp, axis=1, keepdims=True)
    weighted = jnp.dot(resp.astype(jnp.bfloat16), pts, preferred_element_type=jnp.float32)
    fresh = (weighted + PRIOR_ONE * cen.astype(jnp.float32)) * (1.0 / (mass + PRIOR_ONE))
    one_ref[...] = fresh.astype(jnp.bfloat16)
    moved_ref[...] = (mass * fresh).astype(jnp.bfloat16)
    mass_ref[...] = jnp.broadcast_to(mass, (tile, LANES)).T[0:1, :]


def coarse_kernel(
    n,
    moved_hbm,
    mass_ref,
    assign_ref,
    init_ref,
    two_ref,
    moved,
    core_out,
    core_in,
    line_out,
    line_in,
    total,
    pair_out,
    pair_in,
    moved_sem,
    core_sem,
    line_sem,
    pair_sem,
):
    group, me = lax.axis_index("groups"), lax.axis_index("cent")
    own, width = init_ref.shape
    lines = n // 4
    line, pair, core = me // 4, lax.rem(me // 2, 2), lax.rem(me, 2)

    def at(z, y, c):
        return (group, z * 4 + y * 2 + c)

    load = pltpu.make_async_copy(moved_hbm, moved, moved_sem)
    load.start()
    barrier = pltpu.get_barrier_semaphore()

    def greet(who):
        pl.semaphore_signal(barrier, inc=1, device_id=who, device_id_type=MESH)

    greet(at(line, pair, 1 - core))
    greet(at(line, 1 - pair, core))

    @pl.loop(1, lines)
    def _(off):
        greet(at(lax.rem(line + off, lines), pair, core))

    pl.semaphore_wait(barrier, lines + 1)
    load.wait()

    lane = lax.broadcasted_iota(jnp.int32, (2 * own, LANES), 1)

    def partial(z, c):
        base = z * (4 * own) + c * own
        row = lax.broadcasted_iota(jnp.int32, (2 * own, 1), 0)
        row = jnp.where(row >= own, row + own, row)
        hit = (assign_ref[...] - base) == row
        weight = jnp.sum(jnp.where(hit, mass_ref[...], 0.0), axis=1, keepdims=True)
        onehot = jnp.where(hit, 1.0, 0.0).astype(jnp.bfloat16)
        return jnp.dot(onehot, moved[...], preferred_element_type=jnp.float32), weight

    def put(dst, sums, weight):
        high = weight.astype(jnp.bfloat16).astype(jnp.float32)
        low = weight - high
        at_lane = lane[: weight.shape[0]]
        tail = jnp.where(at_lane == 0, high, jnp.where(at_lane == 1, low, 0.0))
        dst[:, :width] = sums.astype(jnp.bfloat16)
        dst[:, width:] = tail.astype(jnp.bfloat16)

    def get(src):
        tail = src[:, width:].astype(jnp.float32)
        return src[:, :width].astype(jnp.float32), jnp.sum(tail, axis=1, keepdims=True)

    def core_copy(s):
        return pltpu.make_async_remote_copy(
            src_ref=core_out.at[s],
            dst_ref=core_in.at[s],
            send_sem=core_sem.at[0, s],
            recv_sem=core_sem.at[1, s],
            device_id=at(line, pair, 1 - core),
            device_id_type=MESH,
        )

    def line_copy(s):
        return pltpu.make_async_remote_copy(
            src_ref=line_out.at[s],
            dst_ref=line_in.at[s],
            send_sem=line_sem.at[0, s],
            recv_sem=line_sem.at[1, s],
            device_id=at(lax.rem(line + 1 + s, lines), pair, core),
            device_id_type=MESH,
        )

    @pl.loop(0, lines)
    def _(s):
        z = lax.rem(line + 1 + s, lines)
        put(core_out.at[s], *partial(z, 1 - core))
        core_copy(s).start()
        sums, weight = partial(z, core)
        total[:, :width] = sums
        core_copy(s).wait_recv()
        other, other_weight = get(core_in.at[s])
        sums = total[:, :width] + other
        weight = weight + other_weight

        @pl.when(s < lines - 1)
        def _():
            put(line_out.at[s], sums, weight)
            line_copy(s).start()

        @pl.when(s == lines - 1)
        def _():
            total[:, :width] = sums
            total[:, width:] = jnp.broadcast_to(weight, (2 * own, LANES))

    @pl.loop(0, lines - 1)
    def _(s):
        line_copy(s).wait_recv()
        sums, weight = get(line_in.at[s])
        total[:, :width] = total[:, :width] + sums
        total[:, width:] = total[:, width:] + weight

    def half(y):
        rows = pl.ds(pl.multiple_of(y * own, own), own)
        return total[rows, :width], total[rows, width : width + 1]

    put(pair_out, *half(1 - pair))
    swap = pltpu.make_async_remote_copy(
        src_ref=pair_out,
        dst_ref=pair_in,
        send_sem=pair_sem.at[0],
        recv_sem=pair_sem.at[1],
        device_id=at(line, 1 - pair, core),
        device_id_type=MESH,
    )
    swap.start()
    swap.wait_recv()
    sums, weight = half(pair)
    other, other_weight = get(pair_in)
    weight = weight + other_weight
    two_ref[...] = (sums + other + PRIOR_TWO * init_ref[...]) / (weight + PRIOR_TWO)

    @pl.loop(0, lines)
    def _(s):
        core_copy(s).wait_send()

    @pl.loop(0, lines - 1)
    def _(s):
        line_copy(s).wait_send()

    swap.wait_send()


def shards(n, points, centroids, coarse_init, assign):
    rows, width = points.shape
    local = centroids.shape[0]
    own = coarse_init.shape[0]
    count = n * rows
    tile = min(512, local)
    vmem = pl.BlockSpec(memory_space=pltpu.VMEM)
    anywhere = pl.BlockSpec(memory_space=pl.ANY)
    everyone, lse = pl.pallas_call(
        functools.partial(stats_kernel, n, tile),
        out_shape=(
            jax.ShapeDtypeStruct((count, width), jnp.bfloat16),
            jax.ShapeDtypeStruct((1, count), jnp.float32),
        ),
        in_specs=[vmem, anywhere],
        out_specs=(vmem, vmem),
        scratch_shapes=[
            pltpu.VMEM((local, width), jnp.bfloat16),
            pltpu.VMEM((2, count), jnp.float32),
            pltpu.VMEM((n - 1, 2, count), jnp.float32),
            pltpu.SemaphoreType.DMA((local // tile,)),
            pltpu.SemaphoreType.DMA((4,)),
        ],
        compiler_params=pltpu.CompilerParams(collective_id=0, has_side_effects=True),
        name="stats",
    )(points, centroids)
    level_one, moved, mass = pl.pallas_call(
        update_kernel,
        grid=(local // tile,),
        out_shape=(
            jax.ShapeDtypeStruct((local, width), jnp.bfloat16),
            jax.ShapeDtypeStruct((local, width), jnp.bfloat16),
            jax.ShapeDtypeStruct((1, local), jnp.float32),
        ),
        in_specs=[
            pl.BlockSpec((tile, width), lambda t: (t, 0)),
            pl.BlockSpec((count, width), lambda t: (0, 0)),
            pl.BlockSpec((1, count), lambda t: (0, 0)),
        ],
        out_specs=(
            pl.BlockSpec((tile, width), lambda t: (t, 0)),
            pl.BlockSpec((tile, width), lambda t: (t, 0)),
            pl.BlockSpec((1, tile), lambda t: (0, t)),
        ),
        name="update",
    )(centroids, everyone, lse)
    lines = n // 4
    wide = width + LANES
    level_two = pl.pallas_call(
        functools.partial(coarse_kernel, n),
        out_shape=jax.ShapeDtypeStruct((own, width), jnp.float32),
        in_specs=[anywhere, vmem, vmem, vmem],
        out_specs=vmem,
        scratch_shapes=[
            pltpu.VMEM((local, width), jnp.bfloat16),
            pltpu.VMEM((lines, 2 * own, wide), jnp.bfloat16),
            pltpu.VMEM((lines, 2 * own, wide), jnp.bfloat16),
            pltpu.VMEM((lines, 2 * own, wide), jnp.bfloat16),
            pltpu.VMEM((lines, 2 * own, wide), jnp.bfloat16),
            pltpu.VMEM((2 * own, wide), jnp.float32),
            pltpu.VMEM((own, wide), jnp.bfloat16),
            pltpu.VMEM((own, wide), jnp.bfloat16),
            pltpu.SemaphoreType.DMA,
            pltpu.SemaphoreType.DMA((2, lines)),
            pltpu.SemaphoreType.DMA((2, lines)),
            pltpu.SemaphoreType.DMA((2,)),
        ],
        compiler_params=pltpu.CompilerParams(collective_id=1, has_side_effects=True),
        name="coarse",
    )(moved, mass, assign.reshape(1, local), coarse_init)
    return (level_one, level_two)


def solution(mesh):
    return jax.shard_map(
        functools.partial(shards, mesh.shape["cent"]),
        mesh=mesh,
        in_specs=(
            P(("groups", "cent"), None),
            P(("groups", "cent"), None),
            P(("groups", "cent"), None),
            P(("groups", "cent")),
        ),
        out_specs=(P(("groups", "cent"), None), P(("groups", "cent"), None)),
        check_vma=False,
    )
```

time: 237 us -> 109 us (0.46); the launches traced: 234 us -> 109 us
  Pallas kernels: 0 us -> 106 us
  blocking collectives: 105 us -> 0 us
  waiting for transfers between devices: 53 us -> 0 us
  matrix products: 49.1 us -> 0 us
  between operations: 14.8 us -> 0.65 us
  other arithmetic: 11.3 us -> 0 us
    pallas_call x0 -> x3, Pallas kernels: none -> 106 us  [the longest x1 57.6 us: shards(): pl.pallas_call(functools.partial(coarse_kernel, n), out_shape=jax.ShapeDt...]
    reduce_scatter x1 -> x0, waiting for transfers between devices: 53 us -> none  [shards(): lax.psum_scatter(wsum_term, 'cent', scatter_dimension=0, tiled=True)]
    dot_general x4 -> x0, matrix products: 49.1 us -> none  [the longest x1 22.7 us: shards(): lax.dot_general(onehot, moved, (((0,), (0,)), ((), ())), preferred_elemen...]
    unnamed x1 -> x0, blocking collectives: 29.9 us -> none
    psum x1 -> x0, blocking collectives: 29.5 us -> none  [shards(): total = lax.psum(local_sum * jnp.exp(local_top - peak), 'cent')]
    pmax x1 -> x0, blocking collectives: 24.7 us -> none  [shards(): peak = lax.pmax(local_top, 'cent')]
    all_gather x1 -> x0, blocking collectives: 21.3 us -> none  [shards(): everyone = lax.all_gather(points, 'cent', axis=0, tiled=True)]
    reduce_sum x2 -> x0, other arithmetic: 9.34 us -> none  [the longest x1 4.88 us: local_stats(): return (top, jnp.sum(jnp.exp(logits - top[:, None]), axis=1))]
  transfers between devices with their start and end apart: 1 -> 0, of which waited for: 1 -> 0; matrix products, arithmetic and copies ran while one was open for 3% -> 0% of each run, Pallas kernels for 0% -> 0%
where the time goes in v1:
time: 109 us
  Pallas kernels  106 us (97%)
  local copies, waits for them, and re-layouts  1.77 us (2%)
    pallas_call x1, Pallas kernels, shards(): pl.pallas_call(functools.partial(coarse_kernel, n), out_shape=jax.ShapeDt...  57.6 us
    pallas_call x1, Pallas kernels, shards(): pl.pallas_call(functools.partial(stats_kernel, n, tile), out_shape=(jax.S...  35 us
    pallas_call x1, Pallas kernels, shards(): pl.pallas_call(update_kernel, grid=(local // tile,), out_shape=(jax.Shape...  13.8 us

profile of v1, /device:TPU:10, one launch (start us, length us, event | category | flops | bytes accessed | tf_op | source)
XLA Modules:
  0.0 108.7 jit_solution(11141153494256438545)
XLA Ops:
  0.6 35.0 %stats.1 = (bf16[512,768]{1,0:T(8,128)(2,1)}, f32[1,512]{1,0:T(1,128)}) custom-call(bf16[32,768]{1,0:T(8,128)(2,1)} %pts_ref.1, bf16[4096,768]{1,0:T(8,128)(2,1)} %cen_ref.1), custom_call_target="tpu_custom_call" | custom-call | tf_op jit(solution)/shard_map/stats/pallas_call | solution.py:275
  35.6 13.8 %update.1 = (bf16[4096,768]{1,0:T(8,128)(2,1)}, bf16[4096,768]{1,0:T(8,128)(2,1)}, f32[1,4096]{1,0:T(1,128)}) custom-call(bf16[4096,768]{1,0:T(8,128)(2,1)} %cen_ref.1, bf16[512,768]{1,0:T(8,128)(2,1)} %get-tuple-element.7.pts_ref, f32[1,512]{1,0:T(1,128)} %get-tuple-element.8.lse_ref), custom_call_target="tpu_custom_call" | custom-call | tf_op jit(solution)/shard_map/update/pallas_call | solution.py:293
  49.4 57.6 %coarse.1 = f32[128,768]{1,0:T(8,128)} custom-call(bf16[4096,768]{1,0:T(8,128)(2,1)} %get-tuple-element.10.moved_hbm, f32[1,4096]{1,0:T(1,128)} %get-tuple-element.11.mass_ref, s32[1,4096]{1,0:T(1,128)} %bitcast.1, f32[128,768]{1,0:T(8,128)} %init_ref.1), custom_call_target="tpu_custom_call" | custom-call | tf_op jit(solution)/shard_map/coarse/pallas_call | solution.py:315
  107.0 1.8 %copy.7 = f32[128,768]{1,0:T(8,128)} copy(f32[128,768]{1,0:T(8,128)} %coarse.1) | data formatting | bytes 786432
